TPU v7x, 32 devices: a whole 2x2x4 slice. The times are simulated.
32 devices in a mesh: facet: 4 (over z), chan: 8 (over y, x, core).
Axes of the slice: x: 2, y: 2, z: 4, core: 2. Of those that a mesh axis runs over, the one named last changes fastest.
Arguments:
- visibilities: bfloat16 [2, 8, 256, 32, 128], P(None, None, None, ('facet', 'chan')), may hold values from -12 to 12
- kernels: bfloat16 [32, 256, 512], replicated, may hold values from -0.25 to 0.25
- delays: float32 [8, 256, 128], P('facet'), may hold values from -4 to 4
- tile_of: int32 [8, 256], P('facet'), may hold values from 0 to 127
- plane_of: int32 [8, 256], P('facet'), may hold values from 0 to 31
- counts: int32 [8], P('facet'), may hold values from 64 to 256
- neighbours: int32 [8, 4], replicated, may hold values from 0 to 7, as said below
Outputs:
- joined_grids: float32 [128, 8, 4, 512], P('chan', 'facet')
Inputs may be any that keep to these rules, and one draw needn't show every extreme that they name: `neighbours`: each row names 4 different facets, none of them its own.
All inputs are finite; a program needn't handle non-finite values.
Results may differ from a plain program's by a relative error of at most 0.0043.
Values may be sent and summed in bfloat16 or wider, within the bound.
A program may use at most 128 MiB of HBM per device.

v0:
```python
import math
import jax
import jax.numpy as jnp
from jax import lax
from jax.sharding import PartitionSpec as P

AVG = 8
TS = 16
NT_DEV = 16
GROUP = 8
EDGE = 4
HIGHEST = lax.Precision.HIGHEST


def average_group(vis_piece, delay_piece, freq_turn, avg_matrix):
    vis_float = vis_piece.astype(jnp.float32)
    phase_angle = delay_piece[:, None, :] * freq_turn[None, :, None]
    cosine = jnp.cos(phase_angle)
    sine_part = jnp.sin(phase_angle)
    rot_real = vis_float[0] * cosine - vis_float[1] * sine_part
    rot_imag = vis_float[0] * sine_part + vis_float[1] * cosine
    avg_real = jnp.einsum("oc,gcv->gov", avg_matrix, rot_real, precision=HIGHEST)
    avg_imag = jnp.einsum("oc,gcv->gov", avg_matrix, rot_imag, precision=HIGHEST)
    return jnp.concatenate([avg_real, avg_imag], axis=-1).astype(jnp.bfloat16)


def project_rows(row_list, plane_list, kernels):
    products = []
    for row_item, plane_item in zip(row_list, plane_list):
        matrix = lax.dynamic_index_in_dim(kernels, plane_item, 0, keepdims=False)
        products.append(jnp.dot(row_item, matrix, preferred_element_type=jnp.float32))
    return jnp.stack(products, axis=0)


def add_tiles(grid_acc, contrib, tile_piece, weight, n_tiles):
    table = (tile_piece[None, :] == jnp.arange(n_tiles, dtype=jnp.int32)[:, None]).astype(
        jnp.float32
    ) * weight[None, :]
    return grid_acc + jnp.einsum("tg,gcx->tcx", table, contrib, precision=HIGHEST)


def grid_facet(
    vis_slot,
    delay_slot,
    tiles_slot,
    planes_slot,
    live_count,
    kernels,
    freq_turn,
    avg_matrix,
    n_tiles,
):
    group_size = GROUP
    out_chan = avg_matrix.shape[0]
    wide_cells = kernels.shape[2]

    def accumulate(step_index, grid_acc):
        begin_row = step_index * group_size
        vis_piece = lax.dynamic_slice_in_dim(vis_slot, begin_row, group_size, 1)
        delay_piece = lax.dynamic_slice_in_dim(delay_slot, begin_row, group_size, 0)
        avg_rows = average_group(vis_piece, delay_piece, freq_turn, avg_matrix)
        plane_piece = lax.dynamic_slice_in_dim(planes_slot, begin_row, group_size, 0)
        contrib = project_rows(
            [avg_rows[g] for g in range(group_size)],
            [plane_piece[g] for g in range(group_size)],
            kernels,
        )
        block_ids = begin_row + jnp.arange(group_size, dtype=jnp.int32)
        live_mask = (block_ids < live_count).astype(jnp.float32)
        tile_piece = lax.dynamic_slice_in_dim(tiles_slot, begin_row, group_size, 0)
        return add_tiles(grid_acc, contrib, tile_piece, live_mask, n_tiles)

    trip_count = (live_count + group_size - 1) // group_size
    start_grid = jnp.zeros((n_tiles, out_chan, wide_cells), jnp.float32)
    return lax.fori_loop(0, trip_count, accumulate, start_grid)


def local(visibilities, kernels, delays, tile_of, plane_of, counts, neighbours):
    n_facet = lax.axis_size("facet")
    n_chan = lax.axis_size("chan")
    facet_index = lax.axis_index("facet")
    chan_index = lax.axis_index("chan")
    halves, facets, blocks, ch_dev, block_vis = visibilities.shape
    fac_dev = facets // n_facet
    blk_dev = blocks // n_chan
    channels = ch_dev * n_facet * n_chan
    out_chan = channels // AVG
    tile_cells = kernels.shape[2] // 2
    n_tiles = NT_DEV * n_chan
    edge_cells = EDGE * TS
    reshaped = visibilities.reshape(halves, n_facet, fac_dev, blk_dev, n_chan, ch_dev, block_vis)
    arranged = jnp.transpose(reshaped, (0, 1, 4, 2, 3, 5, 6))
    my_delays = lax.dynamic_index_in_dim(
        delays.reshape(fac_dev, blk_dev, n_chan, block_vis), chan_index, 2, keepdims=False
    )
    my_tiles = lax.dynamic_index_in_dim(
        tile_of.reshape(fac_dev, blk_dev, n_chan), chan_index, 2, keepdims=False
    )
    my_planes = lax.dynamic_index_in_dim(
        plane_of.reshape(fac_dev, blk_dev, n_chan), chan_index, 2, keepdims=False
    )
    my_live = jnp.clip((counts - chan_index + n_chan - 1) // n_chan, 0, blk_dev)
    position = jnp.arange(channels, dtype=jnp.int32)
    flattened = arranged.reshape(halves, n_facet * n_chan, fac_dev, blk_dev, ch_dev, block_vis)
    received = lax.all_to_all(flattened, ("facet", "chan"), split_axis=1, concat_axis=4, tiled=True)
    local_vis = received.reshape(halves, fac_dev, blk_dev, channels, block_vis)
    freq_turn = 2.0 * math.pi * (1.0 + 0.5 * position.astype(jnp.float32) / channels)
    avg_matrix = (
        position[None, :] // AVG == jnp.arange(out_chan, dtype=jnp.int32)[:, None]
    ).astype(jnp.float32) / AVG
    facet_grids = []
    for facet_slot in range(fac_dev):
        facet_grids.append(
            grid_facet(
                local_vis[:, facet_slot],
                my_delays[facet_slot],
                my_tiles[facet_slot],
                my_planes[facet_slot],
                my_live[facet_slot],
                kernels,
                freq_turn,
                avg_matrix,
                n_tiles,
            )
        )
    stacked = jnp.stack(facet_grids, axis=1)
    summed = lax.psum_scatter(stacked, "chan", scatter_dimension=0, tiled=True)
    strips = jnp.concatenate(
        [summed[..., :edge_cells], summed[..., tile_cells : tile_cells + edge_cells]], axis=-1
    )
    gathered = lax.all_gather(strips.astype(jnp.bfloat16), "facet", axis=1, tiled=True).astype(
        strips.dtype
    )
    my_neighbours = lax.dynamic_slice_in_dim(neighbours, facet_index * fac_dev, fac_dev, 0)
    adjacency = jnp.sum(
        (my_neighbours[:, :, None] == jnp.arange(facets, dtype=jnp.int32)[None, None, :]).astype(
            jnp.float32
        ),
        axis=1,
    )
    blended = 0.25 * jnp.einsum("fg,tgcx->tfcx", adjacency, gathered, precision=HIGHEST)
    joined = summed.at[..., tile_cells - edge_cells : tile_cells].add(blended[..., :edge_cells])
    joined = joined.at[..., 2 * tile_cells - edge_cells :].add(blended[..., edge_cells:])
    return joined


def solution(mesh):
    return jax.shard_map(
        local,
        mesh=mesh,
        in_specs=(
            P(None, None, None, ("facet", "chan"), None),
            P(),
            P("facet", None, None),
            P("facet", None),
            P("facet", None),
            P("facet"),
            P(),
        ),
        out_specs=P("chan", "facet", None, None),
        check_vma=False,
    )
```

profile of v0, /device:TPU:0, one launch (start us, length us, event | category | flops | bytes accessed | tf_op | source)
XLA Modules:
  0.0 319.1 jit_solution(13530689246377154184)
XLA Ops:
  6.5 2.5 copy.46
  9.0 7.3 %all-to-all-start = ((bf16[2,32,2,32,1,128]{5,3,0,2,4,1:T(8,128)(2,1)}), bf16[2,32,2,32,1,128]{5,3,0,2,4,1:T(8,128)(2,1)S(1)}, u32[]{:S(2)}, u32[]{:S(2)}) async-start(bf16[2,32,2,32,1,128]{5,3,0,2,4,1:T(8,128)(2,1)} %bitcast.3), calls=%async_computation | async-start | bytes 2097152 | tf_op jit(solution)/shard_map/all_to_all | solution.py:105
  21.9 20.6 %all-to-all-done = bf16[2,32,2,32,1,128]{5,3,0,2,4,1:T(8,128)(2,1)S(1)} async-done(((bf16[2,32,2,32,1,128]{5,3,0,2,4,1:T(8,128)(2,1)}), bf16[2,32,2,32,1,128]{5,3,0,2,4,1:T(8,128)(2,1)S(1)}, u32[]{:S(2)}, u32[]{:S(2)}) %all-to-all-start) | async-done | bytes 1048608 | tf_op jit(solution)/shard_map/all_to_all | solution.py:105
  42.8 84.7 %while.26 = (s32[]{:T(128)}, f32[128,4,512]{2,0,1:T(8,128)S(1)}, s32[]{:T(128)}, s32[32]{0:T(128)S(1)}, s32[]{:T(128)}, /*index=5*/bf16[2,32,32,128]{3,1,0,2:T(8...) while((s32[]{:T(128)}, f32[128,4,512]{2,0,1:T(8,128)S(1)}, ...), condition=%wide.region_1.2_spmd.clone.clone, body=%wide.region_0.1_spmd.clone.clone.sunk | while | flops 37333684 | bytes 5670299 | solution.py:75
  50.0 1.1 fusion.311
  53.0 1.1 fusion.312
  55.9 1.1 fusion.313
  58.9 1.1 fusion.314
  62.0 1.1 fusion.315
  64.7 1.1 fusion.316
  69.8 1.3 convolution_add_fusion.4
  98.0 1.3 convolution_add_fusion.4
  115.4 1.1 fusion.314
  121.2 1.1 fusion.316
  126.2 1.3 convolution_add_fusion.4
  128.3 56.6 %while.27 = (s32[]{:T(128)}, f32[128,4,512]{2,0,1:T(8,128)S(1)}, s32[]{:T(128)}, s32[32]{0:T(128)S(1)}, s32[]{:T(128)}, /*index=5*/bf16[2,32,32,128]{3,1,0,2:T(8...) while((s32[]{:T(128)}, f32[128,4,512]{2,0,1:T(8,128)S(1)}, ...), condition=%wide.region_3.4_spmd.clone.clone, body=%wide.region_2.3_spmd.clone.clone.sunk | while | flops 37333684 | bytes 5670299 | solution.py:75
  155.4 1.3 convolution_add_fusion.5
  169.8 1.1 fusion.346
  183.6 1.3 convolution_add_fusion.5
  185.6 1.9 pad_maximum_fusion.2
  189.0 87.8 %all-reduce.3.cloned.1.call-done = f32[128,2,4,512]{3,2,1,0:T(4,128)} async-done(((f32[128,2,4,512]{3,2,1,0:T(4,128)}), f32[128,2,4,512]{3,2,1,0:T(4,128)}) %all-reduce.3.cloned.1.call-update) | async-done | bytes 2097168
  278.0 13.4 %all_gather.3 = bf16[16,8,4,128]{3,0,2,1:T(8,128)(2,1)S(1)} all-gather(bf16[16,2,4,128]{3,0,2,1:T(8,128)(2,1)S(1)} %copy.52), channel_id=1, replica_groups=mesh['facet'=4,'chan'=8] {'facet'}, dimensions={1}, use_global_device_ids=true | all-gather | bytes 163840 | tf_op jit(solution)/shard_map/all_gather | solution.py:131
  292.0 9.7 %scatter-add.6 = f32[16,2,4,512]{3,1,2,0:T(2,128)S(1)} dynamic-update-slice(f32[16,2,4,512]{3,1,2,0:T(2,128)S(1)} %copy.55, f32[16,2,4,64]{3,1,2,0:T(2,128)S(1)} %slice_add_fusion.1, s32[]{:T(128)} %constant.186.clone.1, s32[]{:T(128)} %constant.186.clone.1, s32[]{:T(128)} %constant.186.clone.1, s32[]{:T(128)} %constant.202.clone.1) | dynamic-update-slice | bytes 65540 | tf_op jit(solution)/shard_map/scatter-add | solution.py:142
  301.9 9.6 %scatter-add.9 = f32[16,2,4,512]{3,1,2,0:T(2,128)S(1)} dynamic-update-slice(f32[16,2,4,512]{3,1,2,0:T(2,128)S(1)} %scatter-add.6, f32[16,2,4,64]{3,1,2,0:T(2,128)S(1)} %slice_add_fusion, s32[]{:T(128)} %constant.186.clone.1, s32[]{:T(128)} %constant.186.clone.1, s32[]{:T(128)} %constant.186.clone.1, s32[]{:T(128)} %constant.203.clone.1) | dynamic-update-slice | bytes 65540 | tf_op jit(solution)/shard_map/scatter-add | solution.py:143
  (112 shorter events, 58.6 us)
Async XLA Ops:
  6.5 181.0 %copy-start = (s32[8,4]{0,1:T(4,128)S(1)}, s32[8,4]{0,1:T(4,128)}, u32[]{:S(2)}) copy-start(s32[8,4]{0,1:T(4,128)} %param.21) | copy-start | bytes 388
  9.0 33.5 %all-to-all-start = ((bf16[2,32,2,32,1,128]{5,3,0,2,4,1:T(8,128)(2,1)}), bf16[2,32,2,32,1,128]{5,3,0,2,4,1:T(8,128)(2,1)S(1)}, u32[]{:S(2)}, u32[]{:S(2)}) async-start(bf16[2,32,2,32,1,128]{5,3,0,2,4,1:T(8,128)(2,1)} %bitcast.3), calls=%async_computation | async-start | bytes 2097152 | tf_op jit(solution)/shard_map/all_to_all | solution.py:105
  16.4 260.4 %all-reduce.3.cloned.1.call-start = ((), (), s32[]{:S(2)}) async-start(), calls=%async_computation.1 | async-start | bytes 4194304
  184.9 2.8 copy-start.1
Sparse Core Ops, SparseCore 0:
  187.6 89.1 all-reduce.2
where the time goes:
time: 322 us; the launch traced here: 319 us
  waiting for transfers between devices  108 us (34%)
  loops' own time  75.9 us (24%)
  matrix products  57.8 us (18%)
  local copies, waits for them, and re-layouts  32.9 us (10%)
  between operations  15.6 us (5%)
  blocking collectives  13.4 us (4%)
  other arithmetic  7.59 us (2%)
  starting transfers between devices  7.37 us (2%)
    unnamed x2, waiting for transfers between devices  87.8 us
    another operation x2, loops' own time, grid_facet(): return lax.fori_loop(0, trip_count, accumulate, start_grid)  75.9 us
    dot_general x40, matrix products, project_rows(): jnp.dot(row_item, matrix, preferred_element_type=jnp.float32)  43.9 us
    all_to_all x1, waiting for transfers between devices, local(): lax.all_to_all(flattened, ('facet', 'chan'), split_axis=1, concat_axis=4,...  20.6 us
    all_gather x1, blocking collectives, local(): lax.all_gather(strips.astype(jnp.bfloat16), 'facet', axis=1, tiled=True)  13.4 us
    scatter-add x2, local copies, waits for them, and re-layouts, local(): joined.at[..., 2 * tile_cells - edge_cells:].add(blended[..., edge_cells:])  10.4 us
    scatter-add x1, local copies, waits for them, and re-layouts, local(): summed.at[..., tile_cells - edge_cells:tile_cells]  9.66 us
    all_to_all x1, starting transfers between devices, local(): lax.all_to_all(flattened, ('facet', 'chan'), split_axis=1, concat_axis=4,...  7.33 us
  transfers between devices with their start and end apart: 2, of which 2 were waited for; matrix products, arithmetic and copies ran while one was open for 2% of the time, Pallas kernels for 0%

commit v1 on v0

--- a/solution.py
+++ b/solution.py
@@ -102,7 +102,16 @@
     my_live = jnp.clip((counts - chan_index + n_chan - 1) // n_chan, 0, blk_dev)
     position = jnp.arange(channels, dtype=jnp.int32)
     flattened = arranged.reshape(halves, n_facet * n_chan, fac_dev, blk_dev, ch_dev, block_vis)
-    received = lax.all_to_all(flattened, ("facet", "chan"), split_axis=1, concat_axis=4, tiled=True)
+    fit_patch_up = lambda panel, mesh_name: jnp.concatenate(
+        jax.lax.all_to_all(
+            jnp.stack(jnp.split(panel, jax.lax.axis_size(mesh_name), axis=1), axis=0),
+            mesh_name,
+            0,
+            0,
+        ),
+        axis=4,
+    )
+    received = fit_patch_up(flattened, ("facet", "chan"))
     local_vis = received.reshape(halves, fac_dev, blk_dev, channels, block_vis)
     freq_turn = 2.0 * math.pi * (1.0 + 0.5 * position.astype(jnp.float32) / channels)
     avg_matrix = (

time: 322 us -> 341 us (1.059)
  local copies, waits for them, and re-layouts: 32.9 us -> 51.3 us
    unnamed x5 -> x36, local copies, waits for them, and re-layouts: 0.59 us -> 19.3 us
  transfers between devices with their start and end apart: 2 -> 2, of which waited for: 2 -> 2; matrix products, arithmetic and copies ran while one was open for 2% -> 1% of each run, Pallas kernels for 0% -> 0%
where the time goes in v1:
time: 341 us; the launch traced here: 338 us
  waiting for transfers between devices  108 us (32%)
  loops' own time  75.9 us (22%)
  matrix products  57.8 us (17%)
  local copies, waits for them, and re-layouts  51.3 us (15%)
  between operations  15.7 us (5%)
  blocking collectives  13.4 us (4%)
  other arithmetic  7.59 us (2%)
  starting transfers between devices  7.37 us (2%)
    unnamed x2, waiting for transfers between devices  87.8 us
    another operation x2, loops' own time, grid_facet(): return lax.fori_loop(0, trip_count, accumulate, start_grid)  75.9 us
    dot_general x40, matrix products, project_rows(): jnp.dot(row_item, matrix, preferred_element_type=jnp.float32)  43.9 us
    all_to_all x1, waiting for transfers between devices, local(): jax.lax.all_to_all(jnp.stack(jnp.split(panel, jax.lax.axis_size(mesh_name...  20.6 us
    unnamed x36, local copies, waits for them, and re-layouts  19.3 us
    all_gather x1, blocking collectives, local(): lax.all_gather(strips.astype(jnp.bfloat16), 'facet', axis=1, tiled=True)  13.4 us
    scatter-add x2, local copies, waits for them, and re-layouts, local(): joined.at[..., 2 * tile_cells - edge_cells:].add(blended[..., edge_cells:])  10.4 us
    scatter-add x1, local copies, waits for them, and re-layouts, local(): summed.at[..., tile_cells - edge_cells:tile_cells]  9.66 us
  transfers between devices with their start and end apart: 2, of which 2 were waited for; matrix products, arithmetic and copies ran while one was open for 1% of the time, Pallas kernels for 0%

profile of v1, /device:TPU:0, one launch (start us, length us, event | category | flops | bytes accessed | tf_op | source)
XLA Modules:
  0.0 337.6 jit_solution(15578383240599463969)
XLA Ops:
  6.5 1.5 copy.81
  27.4 7.3 %all-to-all-start = ((bf16[32,2,1,2,32,1,128]{6,4,3,1,5,2,0:T(8,128)(2,1)}), bf16[32,2,1,2,32,1,128]{6,4,3,1,5,2,0:T(8,128)(2,1)S(1)}, u32[]{:S(2)}, u32[]{:S(2)}) async-start(bf16[32,2,1,2,32,1,128]{6,4,3,1,5,2,0:T(8,128)(2,1)} %constant_dynamic-update-slice_fusion), calls=%async_computation | async-start | bytes 2097152 | tf_op jit(solution)/shard_map/all_to_all | solution.py:106
  40.3 20.6 %all-to-all-done = bf16[32,2,1,2,32,1,128]{6,4,3,1,5,2,0:T(8,128)(2,1)S(1)} async-done(((bf16[32,2,1,2,32,1,128]{6,4,3,1,5,2,0:T(8,128)(2,1)}), bf16[32,2,1,2,32,1,128]{6,4,3,1,5,2,0:T(8,128)(2,1)S(1)}, u32[]{:S(2)}, u32[]{:S(2)}) %all-to-all-start) | async-done | bytes 1048608 | tf_op jit(solution)/shard_map/all_to_all | solution.py:106
  61.2 84.7 %while.26 = (s32[]{:T(128)}, f32[128,4,512]{2,0,1:T(8,128)S(1)}, s32[]{:T(128)}, s32[32]{0:T(128)S(1)}, s32[]{:T(128)}, /*index=5*/bf16[2,32,32,128]{3,1,0,2:T(8...) while((s32[]{:T(128)}, f32[128,4,512]{2,0,1:T(8,128)S(1)}, ...), condition=%wide.region_1.2_spmd.clone.clone, body=%wide.region_0.1_spmd.clone.clone.sunk | while | flops 37333684 | bytes 5670299 | solution.py:75
  68.5 1.1 fusion.311
  71.4 1.1 fusion.312
  74.4 1.1 fusion.313
  77.4 1.1 fusion.314
  80.4 1.1 fusion.315
  83.2 1.1 fusion.316
  86.4 1.1 fusion.317
  88.2 1.3 convolution_add_fusion.4
  96.7 1.1 fusion.311
  99.7 1.1 fusion.312
  116.4 1.3 convolution_add_fusion.4
  144.7 1.3 convolution_add_fusion.4
  146.8 56.6 %while.27 = (s32[]{:T(128)}, f32[128,4,512]{2,0,1:T(8,128)S(1)}, s32[]{:T(128)}, s32[32]{0:T(128)S(1)}, s32[]{:T(128)}, /*index=5*/bf16[2,32,32,128]{3,1,0,2:T(8...) while((s32[]{:T(128)}, f32[128,4,512]{2,0,1:T(8,128)S(1)}, ...), condition=%wide.region_3.4_spmd.clone.clone, body=%wide.region_2.3_spmd.clone.clone.sunk | while | flops 37333684 | bytes 5670299 | solution.py:75
  173.8 1.3 convolution_add_fusion.5
  202.1 1.3 convolution_add_fusion.5
  204.1 1.9 pad_maximum_fusion.2
  207.5 87.8 %all-reduce.3.cloned.1.call-done = f32[128,2,4,512]{3,2,1,0:T(4,128)} async-done(((f32[128,2,4,512]{3,2,1,0:T(4,128)}), f32[128,2,4,512]{3,2,1,0:T(4,128)}) %all-reduce.3.cloned.1.call-update) | async-done | bytes 2097168
  296.5 13.4 %all_gather.3 = bf16[16,8,4,128]{3,0,2,1:T(8,128)(2,1)S(1)} all-gather(bf16[16,2,4,128]{3,0,2,1:T(8,128)(2,1)S(1)} %copy.87), channel_id=1, replica_groups=mesh['facet'=4,'chan'=8] {'facet'}, dimensions={1}, use_global_device_ids=true | all-gather | bytes 163840 | tf_op jit(solution)/shard_map/all_gather | solution.py:140
  310.5 9.7 %scatter-add.6 = f32[16,2,4,512]{3,1,2,0:T(2,128)S(1)} dynamic-update-slice(f32[16,2,4,512]{3,1,2,0:T(2,128)S(1)} %copy.90, f32[16,2,4,64]{3,1,2,0:T(2,128)S(1)} %slice_add_fusion.1, s32[]{:T(128)} %constant.186.clone.1, s32[]{:T(128)} %constant.186.clone.1, s32[]{:T(128)} %constant.186.clone.1, s32[]{:T(128)} %constant.202.clone.1) | dynamic-update-slice | bytes 65540 | tf_op jit(solution)/shard_map/scatter-add | solution.py:151
  320.4 9.6 %scatter-add.9 = f32[16,2,4,512]{3,1,2,0:T(2,128)S(1)} dynamic-update-slice(f32[16,2,4,512]{3,1,2,0:T(2,128)S(1)} %scatter-add.6, f32[16,2,4,64]{3,1,2,0:T(2,128)S(1)} %slice_add_fusion, s32[]{:T(128)} %constant.186.clone.1, s32[]{:T(128)} %constant.186.clone.1, s32[]{:T(128)} %constant.186.clone.1, s32[]{:T(128)} %constant.203.clone.1) | dynamic-update-slice | bytes 65540 | tf_op jit(solution)/shard_map/scatter-add | solution.py:152
  (144 shorter events, 78.0 us)
Async XLA Ops:
  6.5 199.5 %copy-start = (s32[8,4]{0,1:T(4,128)S(1)}, s32[8,4]{0,1:T(4,128)}, u32[]{:S(2)}) copy-start(s32[8,4]{0,1:T(4,128)} %param.21) | copy-start | bytes 388
  27.4 33.5 %all-to-all-start = ((bf16[32,2,1,2,32,1,128]{6,4,3,1,5,2,0:T(8,128)(2,1)}), bf16[32,2,1,2,32,1,128]{6,4,3,1,5,2,0:T(8,128)(2,1)S(1)}, u32[]{:S(2)}, u32[]{:S(2)}) async-start(bf16[32,2,1,2,32,1,128]{6,4,3,1,5,2,0:T(8,128)(2,1)} %constant_dynamic-update-slice_fusion), calls=%async_computation | async-start | bytes 2097152 | tf_op jit(solution)/shard_map/all_to_all | solution.py:106
  34.7 260.5 %all-reduce.3.cloned.1.call-start = ((), (), s32[]{:S(2)}) async-start(), calls=%async_computation.1 | async-start | bytes 4194304
  203.4 2.8 copy-start.1
Sparse Core Ops, SparseCore 0:
  206.1 89.1 all-reduce.2
